TPU v7x, 256 devices: a whole 4x4x8 slice. The times are simulated.
256 devices in a mesh: grp: 16 (over x, y_hi, core), rng: 16 (over z, y_lo).
Axes of the slice: x: 4, y: 4 (y_hi: 2, y_lo: 2; y = y_hi * 2 + y_lo), z: 8, core: 2. Of those that a mesh axis runs over, the one named last changes fastest.
Arguments:
- features: bfloat16 [65536, 1024], P(('grp', 'rng')), may hold values from -6 to 6
- query_weight: bfloat16 [1024, 1024], replicated
- key_weight: bfloat16 [1024, 1024], replicated
- value_weight: bfloat16 [1024, 1024], replicated, may hold values from -0.1875 to 0.1875
- out_weight: bfloat16 [1024, 1024], replicated, may hold values from -0.1875 to 0.1875
- band_reach: int32 [256], P(('grp', 'rng')), may hold values from 16 to 128, as said below
- long_peers: int32 [512, 6], P(('grp', 'rng')), may hold values from 0 to 15, as said below
- long_count: int32 [512], P(('grp', 'rng')), may hold values from 0 to 6, as said below
- send_tile: int32 [256, 16], P(('grp', 'rng')), may hold values from 0 to 3
Outputs:
- updated: bfloat16 [65536, 1024], P(('grp', 'rng'))
Inputs may be any that keep to these rules, and one draw needn't show every extreme that they name: `band_reach`: some range has 128 in every draw. `long_peers`: the 6 entries of a query tile in region g are distinct regions other than g; only the first long_count entries are used. `long_count`: some query tile has 6 in every draw.
All inputs are finite; a program needn't handle non-finite values.
Results may differ from a plain program's by a relative error of at most 0.0064.
Values may be sent and summed in bfloat16 or wider, within the bound.
A program may use at most 128 MiB of HBM per device.

v0:
```python
import functools

import jax
import jax.numpy as jnp
from jax import lax
from jax.experimental import pallas as pl
from jax.experimental.pallas import tpu as pltpu
from jax.sharding import PartitionSpec as P

MESH = pl.DeviceIdType.MESH
F32 = jnp.float32
BF16 = jnp.bfloat16

EPSILON = 1e-06
D = 1024
ROWS = 256
TILE = 128
PORTAL = 64
MAXLONG = 6
LANES = 128
PAIRS = D // LANES
SCALE = 64 ** (-0.5)
FLOOR = -3.0e38

GRAY = {0: 0, 1: 1, 2: 3, 3: 2}
X_ORDER = ((1, 0), (3, 0), (1, 1), (3, 1), (2, 0), (2, 1))
NEAR_BLOCKS = 2 * ROWS // PORTAL


def project(src, block, count, weight, dst, dst_block, scale=None):
    @pl.loop(0, D // 256)
    def _(step):
        columns = pl.ds(pl.multiple_of(step * 256, 256), 256)
        total = jnp.dot(
            src[pl.ds(block, count)].reshape(count * PORTAL, D),
            weight[:, columns],
            preferred_element_type=F32,
        ).astype(BF16)
        if scale is not None:
            total = total * jnp.asarray(scale, BF16)
        dst[pl.ds(dst_block, count), :, columns] = total.reshape(count, PORTAL, 256)


def kernel(
    reach_ref,
    peers_ref,
    count_ref,
    pick_ref,
    feat_hbm,
    wq_hbm,
    wk_hbm,
    wv_hbm,
    wo_hbm,
    out_ref,
    feat,
    wq,
    wk,
    wv,
    wo,
    normed,
    partner,
    partner_pick,
    halo,
    arrived,
    stage_own,
    stage_far,
    queries,
    keys,
    values,
    attended,
    bias_near,
    bias_far,
    acc_near,
    sum_near,
    max_near,
    in_sem,
    send_own,
    recv_own,
    send_far,
    recv_far,
    send_y,
    recv_y,
    send_halo,
    recv_halo,
):
    g = lax.axis_index("grp")
    r = lax.axis_index("rng")
    x, row_bit, core = g // 4, (g // 2) % 2, g % 2

    def device(dx, dy, dc):
        return (
            lax.rem(x + dx, 4) * 4 + lax.rem(row_bit + dy, 2) * 2 + lax.rem(core + dc, 2),
            r,
        )

    above = (g, lax.rem(r + 1, 16))
    below = (g, lax.rem(r + 15, 16))
    row_flows = X_ORDER + ((0, 1),)

    loads = [
        pltpu.make_async_copy(src, dst, in_sem.at[i])
        for i, (src, dst) in enumerate(
            ((feat_hbm, feat), (wq_hbm, wq), (wk_hbm, wk), (wv_hbm, wv), (wo_hbm, wo))
        )
    ]
    for load in loads:
        load.start()

    barrier = pltpu.get_barrier_semaphore()
    friends = [device(dx, 0, dc) for dx, dc in row_flows] + [device(0, 1, 0), above, below]
    for friend in friends:
        pl.semaphore_signal(barrier, inc=1, device_id=friend, device_id_type=MESH)

    loads[0].wait()

    @pl.loop(0, ROWS // PORTAL)
    def _(block):
        rows = pl.ds(pl.multiple_of(block * PORTAL, PORTAL), PORTAL)
        widened = feat[rows, :].astype(F32)
        factor = lax.rsqrt(jnp.mean(widened * widened, axis=1, keepdims=True) + EPSILON)
        normed[block] = (widened * factor).astype(BF16)

    def pick_own(flow):
        dx, dc = row_flows[flow]
        target, _ = device(dx, 0, dc)
        stage_own[flow] = normed[pick_ref[0, target]]

    def slot_of_flow(dx, dc, far):
        return 8 * far + 2 * GRAY[dx] + dc

    for flow in range(len(row_flows)):
        pick_own(flow)

    pl.semaphore_wait(barrier, len(friends))

    cross = [
        pltpu.make_async_remote_copy(
            src_ref=normed, dst_ref=partner, send_sem=send_y.at[0], recv_sem=recv_y.at[0],
            device_id=device(0, 1, 0), device_id_type=MESH,
        ),
        pltpu.make_async_remote_copy(
            src_ref=pick_ref, dst_ref=partner_pick, send_sem=send_y.at[1], recv_sem=recv_y.at[1],
            device_id=device(0, 1, 0), device_id_type=MESH,
        ),
    ]
    for copy in cross:
        copy.start()
    own = []
    for flow, (dx, dc) in enumerate(row_flows):
        copy = pltpu.make_async_remote_copy(
            src_ref=stage_own.at[flow],
            dst_ref=arrived.at[slot_of_flow(dx, dc, 0)],
            send_sem=send_own.at[flow],
            recv_sem=recv_own.at[flow],
            device_id=device(dx, 0, dc),
            device_id_type=MESH,
        )
        copy.start()
        own.append(copy)

    reach = reach_ref[0]
    place_q = lax.broadcasted_iota(jnp.int32, (ROWS, ROWS), 0)
    place_k = lax.broadcasted_iota(jnp.int32, (ROWS, ROWS), 1)
    bias_near[...] = jnp.where(jnp.abs(place_q - place_k) <= reach, 0.0, -jnp.inf)
    tile_q = lax.broadcasted_iota(jnp.int32, (TILE, TILE), 0)
    tile_k = lax.broadcasted_iota(jnp.int32, (TILE, TILE), 1)
    slot_of = lax.broadcasted_iota(jnp.int32, (TILE, MAXLONG * PORTAL), 1) // PORTAL
    for tile in range(2):
        gap = (tile_q - tile_k if tile == 0 else tile_k - tile_q) + TILE
        bias_far[tile, :, :TILE] = jnp.where(gap <= reach, 0.0, -jnp.inf)
        bias_far[tile, :, TILE:] = jnp.where(slot_of < count_ref[tile], 0.0, -jnp.inf)

    loads[1].wait()
    project(normed, 0, 4, wq, queries, 0, SCALE)
    loads[2].wait()
    project(normed, 0, 4, wk, keys, 2)
    loads[3].wait()
    project(normed, 0, 4, wv, values, 2)

    even = lax.broadcasted_iota(jnp.int32, (TILE, LANES), 1) < LANES // 2

    def attend(tile, lanes, key_rows, value_rows, bias):
        query = queries[pl.ds(tile * 2, 2), :, lanes].reshape(TILE, LANES)
        none = jnp.zeros_like(query)
        both = jnp.concatenate(
            [jnp.where(even, query, none), jnp.where(even, none, query)], axis=0
        )
        scores = lax.dot_general(
            both, key_rows, (((1,), (1,)), ((), ())), preferred_element_type=F32
        )
        scores = scores + jnp.concatenate([bias, bias], axis=0)
        highest = jnp.maximum(jnp.max(scores, axis=1, keepdims=True), FLOOR)
        weights = jnp.exp(scores - highest).astype(BF16)
        wide = jnp.concatenate([value_rows, jnp.ones_like(value_rows)], axis=1)
        mixed = jnp.dot(weights, wide, preferred_element_type=F32)
        top = jnp.broadcast_to(highest, (2 * TILE, LANES))
        return (
            jnp.where(even, mixed[:TILE, :LANES], mixed[TILE:, :LANES]),
            jnp.where(even, mixed[:TILE, LANES:], mixed[TILE:, LANES:]),
            jnp.where(even, top[:TILE], top[TILE:]),
        )

    @pl.loop(0, PAIRS)
    def _(pair):
        lanes = pl.ds(pl.multiple_of(pair * LANES, LANES), LANES)
        near = pl.ds(2, 4)
        key_rows = keys[near, :, lanes].reshape(ROWS, LANES)
        value_rows = values[near, :, lanes].reshape(ROWS, LANES)
        for tile in range(2):
            rows = pl.ds(tile * TILE, TILE)
            mixed, total, top = attend(
                tile, lanes, key_rows, value_rows, bias_near[rows, :]
            )
            acc_near[rows, lanes] = mixed
            sum_near[rows, lanes] = total
            max_near[rows, lanes] = top

    for copy in own:
        copy.wait_recv()

    def project_slots(first, count):
        project(arrived, first, count, wk, keys, NEAR_BLOCKS + first)
        project(arrived, first, count, wv, values, NEAR_BLOCKS + first)

    project_slots(1, 7)

    for copy in cross:
        copy.wait()

    def far_rows(target):
        return partner[partner_pick[0, target]]

    far = []
    for flow, (dx, dc) in enumerate(row_flows):
        target, _ = device(dx, 0, dc)
        stage_far[flow] = far_rows(target)
    for flow, (dx, dc) in enumerate(row_flows):
        copy = pltpu.make_async_remote_copy(
            src_ref=stage_far.at[flow],
            dst_ref=arrived.at[slot_of_flow(dx, dc, 1)],
            send_sem=send_far.at[flow],
            recv_sem=recv_far.at[flow],
            device_id=device(dx, 0, dc),
            device_id_type=MESH,
        )
        copy.start()
        far.append(copy)
    edges = [
        pltpu.make_async_remote_copy(
            src_ref=normed.at[pl.ds(2, 2)], dst_ref=halo.at[pl.ds(0, 2)],
            send_sem=send_halo.at[0], recv_sem=recv_halo.at[0],
            device_id=above, device_id_type=MESH,
        ),
        pltpu.make_async_remote_copy(
            src_ref=normed.at[pl.ds(0, 2)], dst_ref=halo.at[pl.ds(2, 2)],
            send_sem=send_halo.at[1], recv_sem=recv_halo.at[1],
            device_id=below, device_id_type=MESH,
        ),
    ]
    for copy in edges:
        copy.start()
    arrived[8] = far_rows(g)

    for flow in (6, 0, 1, 2, 3):
        far[flow].wait_recv()
    project_slots(8, 6)
    for copy in edges:
        copy.wait_recv()
    for weight, dst in ((wk, keys), (wv, values)):
        project(halo, 0, 2, weight, dst, 0)
        project(halo, 2, 2, weight, dst, 6)
    for flow in (4, 5):
        far[flow].wait_recv()
    project_slots(14, 2)

    def slot_start(tile, entry):
        peer = peers_ref[tile, entry]
        dx = lax.rem(x + 4 - lax.div(peer, 4), 4)
        place = dx + lax.div(dx, 2) * (1 - 2 * lax.rem(dx, 2))
        other = lax.rem(lax.div(peer, 2) + row_bit, 2)
        turn = lax.rem(peer + core, 2)
        return NEAR_BLOCKS + 8 * other + 2 * place + turn

    for tile in range(2):
        rows = pl.ds(tile * TILE, TILE)
        edge = pl.ds(6 * tile, 2)
        starts = [slot_start(tile, entry) for entry in range(MAXLONG)]

        @pl.loop(0, PAIRS)
        def _(pair):
            lanes = pl.ds(pl.multiple_of(pair * LANES, LANES), LANES)

            def gathered(ref):
                return jnp.concatenate(
                    [ref[edge, :, lanes].reshape(TILE, LANES)]
                    + [ref[start, :, lanes] for start in starts],
                    axis=0,
                )

            mixed, total, top = attend(
                tile, lanes, gathered(keys), gathered(values), bias_far[tile]
            )
            near_top = max_near[rows, lanes]
            highest = jnp.maximum(near_top, top)
            near_part = jnp.exp(near_top - highest)
            far_part = jnp.exp(top - highest)
            mixed = acc_near[rows, lanes] * near_part + mixed * far_part
            total = sum_near[rows, lanes] * near_part + total * far_part
            attended[rows, lanes] = (mixed / total).astype(BF16)

    loads[4].wait()

    @pl.loop(0, D // 256)
    def _(step):
        columns = pl.ds(pl.multiple_of(step * 256, 256), 256)
        total = jnp.dot(attended[...], wo[:, columns], preferred_element_type=F32)
        out_ref[:, columns] = (feat[:, columns].astype(F32) + total).astype(BF16)

    for copy in own + far + edges:
        copy.wait_send()


def local(
    features,
    query_weight,
    key_weight,
    value_weight,
    out_weight,
    band_reach,
    long_peers,
    long_count,
    send_tile,
):
    smem = pl.BlockSpec(memory_space=pltpu.SMEM)
    hbm = pl.BlockSpec(memory_space=pl.ANY)
    flows = len(X_ORDER) + 1
    dma = pltpu.SemaphoreType.DMA
    return pl.pallas_call(
        kernel,
        name="layer",
        out_shape=jax.ShapeDtypeStruct((ROWS, D), BF16),
        in_specs=[smem] * 4 + [hbm] * 5,
        out_specs=pl.BlockSpec(memory_space=pltpu.VMEM),
        scratch_shapes=[
            pltpu.VMEM((ROWS, D), BF16),
            pltpu.VMEM((D, D), BF16),
            pltpu.VMEM((D, D), BF16),
            pltpu.VMEM((D, D), BF16),
            pltpu.VMEM((D, D), BF16),
            pltpu.VMEM((4, PORTAL, D), BF16),
            pltpu.VMEM((4, PORTAL, D), BF16),
            pltpu.SMEM((1, 16), jnp.int32),
            pltpu.VMEM((4, PORTAL, D), BF16),
            pltpu.VMEM((16, PORTAL, D), BF16),
            pltpu.VMEM((flows, PORTAL, D), BF16),
            pltpu.VMEM((flows, PORTAL, D), BF16),
            pltpu.VMEM((4, PORTAL, D), BF16),
            pltpu.VMEM((NEAR_BLOCKS + 16, PORTAL, D), BF16),
            pltpu.VMEM((NEAR_BLOCKS + 16, PORTAL, D), BF16),
            pltpu.VMEM((ROWS, D), BF16),
            pltpu.VMEM((ROWS, ROWS), F32),
            pltpu.VMEM((2, TILE, TILE + MAXLONG * PORTAL), F32),
            pltpu.VMEM((ROWS, D), F32),
            pltpu.VMEM((ROWS, D), F32),
            pltpu.VMEM((ROWS, D), F32),
            dma((5,)),
            dma((flows,)),
            dma((flows,)),
            dma((flows,)),
            dma((flows,)),
            dma((2,)),
            dma((2,)),
            dma((2,)),
            dma((2,)),
        ],
        compiler_params=pltpu.CompilerParams(
            collective_id=0, has_side_effects=True, vmem_limit_bytes=60 * 1024 * 1024
        ),
    )(
        band_reach,
        long_peers,
        long_count,
        send_tile,
        features,
        query_weight,
        key_weight,
        value_weight,
        out_weight,
    )


def solution(mesh):
    return jax.shard_map(
        local,
        mesh=mesh,
        in_specs=(
            P(("grp", "rng"), None),
            P(),
            P(),
            P(),
            P(),
            P(("grp", "rng")),
            P(("grp", "rng"), None),
            P(("grp", "rng")),
            P(("grp", "rng"), None),
        ),
        out_specs=P(("grp", "rng"), None),
        check_vma=False,
    )
```

profile of v0, /device:TPU:17, one launch (start us, length us, event | category | flops | bytes accessed | tf_op | source)
XLA Modules:
  0.0 62.3 jit_solution(11509349484760741857)
XLA Ops:
  0.7 59.8 %layer.1 = bf16[256,1024]{1,0:T(8,128)(2,1)} custom-call(s32[1]{0:T(128)S(6)} %copy.11.reach_ref, s32[2,6]{1,0:T(2,128)} %peers_ref.1, s32[2]{0:T(128)} %count_ref.1, s32[1,16]{1,0:T(1,128)} %pick_ref.1, bf16[256,1024]{1,0:T(8,128)(2,1)} %feat_hbm.1, bf16[1024,1024]{1,0:T(8,128)(2,1)} %wq_hbm.1, bf16[1024,1024]{1,0:T(8,128)(2,1)} %wk_hbm.1, ...), custom_call_target="tpu_custom_call" | custom-call | tf_op jit(solution)/shard_map/layer/pallas_call | solution.py:338
  60.4 1.9 %copy.12 = bf16[256,1024]{1,0:T(8,128)(2,1)} copy(bf16[256,1024]{1,0:T(8,128)(2,1)} %layer.1) | data formatting | bytes 1048576
where the time goes:
time: 62.4 us; the launch traced here: 62.3 us
  Pallas kernels  59.8 us (96%)
  local copies, waits for them, and re-layouts  1.87 us (3%)
  between operations  0.66 us (1%)
    pallas_call x1, Pallas kernels, local(): pl.pallas_call(kernel, name='layer', out_shape=jax.ShapeDtypeStruct((ROWS...  59.8 us
    unnamed x1, local copies, waits for them, and re-layouts  1.87 us

commit v1 on v0

--- a/solution.py
+++ b/solution.py
@@ -24,21 +24,27 @@
 
 GRAY = {0: 0, 1: 1, 2: 3, 3: 2}
 X_ORDER = ((1, 0), (3, 0), (1, 1), (3, 1), (2, 0), (2, 1))
-NEAR_BLOCKS = 2 * ROWS // PORTAL
-
-
-def project(src, block, count, weight, dst, dst_block, scale=None):
-    @pl.loop(0, D // 256)
+NEAR_BLOCKS = 4
+SLOTS = 16
+HALO = NEAR_BLOCKS + SLOTS
+
+
+def project(src, block, count, pairs, dst_block, scale=None):
+    rows = count * PORTAL
+    width = D // 2
+
+    @pl.loop(0, 2, unroll=True)
     def _(step):
-        columns = pl.ds(pl.multiple_of(step * 256, 256), 256)
-        total = jnp.dot(
-            src[pl.ds(block, count)].reshape(count * PORTAL, D),
-            weight[:, columns],
-            preferred_element_type=F32,
-        ).astype(BF16)
-        if scale is not None:
-            total = total * jnp.asarray(scale, BF16)
-        dst[pl.ds(dst_block, count), :, columns] = total.reshape(count, PORTAL, 256)
+        columns = pl.ds(pl.multiple_of(step * width, width), width)
+        for weight, dst in pairs:
+            total = jnp.dot(
+                src[pl.ds(block, count)].reshape(rows, D),
+                weight[:, columns],
+                preferred_element_type=F32,
+            ).astype(BF16)
+            if scale is not None:
+                total = total * jnp.asarray(scale, BF16)
+            dst[pl.ds(dst_block, count), :, columns] = total.reshape(count, PORTAL, width)
 
 
 def kernel(
@@ -60,7 +66,6 @@
     normed,
     partner,
     partner_pick,
-    halo,
     arrived,
     stage_own,
     stage_far,
@@ -171,58 +176,43 @@
         bias_far[tile, :, TILE:] = jnp.where(slot_of < count_ref[tile], 0.0, -jnp.inf)
 
     loads[1].wait()
-    project(normed, 0, 4, wq, queries, 0, SCALE)
+    project(normed, 0, 4, ((wq, queries),), 0, SCALE)
     loads[2].wait()
-    project(normed, 0, 4, wk, keys, 2)
     loads[3].wait()
-    project(normed, 0, 4, wv, values, 2)
+    project(normed, 0, 4, ((wk, keys), (wv, values)), 0)
 
     even = lax.broadcasted_iota(jnp.int32, (TILE, LANES), 1) < LANES // 2
 
     def attend(tile, lanes, key_rows, value_rows, bias):
         query = queries[pl.ds(tile * 2, 2), :, lanes].reshape(TILE, LANES)
         none = jnp.zeros_like(query)
-        both = jnp.concatenate(
-            [jnp.where(even, query, none), jnp.where(even, none, query)], axis=0
-        )
-        scores = lax.dot_general(
-            both, key_rows, (((1,), (1,)), ((), ())), preferred_element_type=F32
-        )
-        scores = scores + jnp.concatenate([bias, bias], axis=0)
-        highest = jnp.maximum(jnp.max(scores, axis=1, keepdims=True), FLOOR)
-        weights = jnp.exp(scores - highest).astype(BF16)
         wide = jnp.concatenate([value_rows, jnp.ones_like(value_rows)], axis=1)
-        mixed = jnp.dot(weights, wide, preferred_element_type=F32)
-        top = jnp.broadcast_to(highest, (2 * TILE, LANES))
-        return (
-            jnp.where(even, mixed[:TILE, :LANES], mixed[TILE:, :LANES]),
-            jnp.where(even, mixed[:TILE, LANES:], mixed[TILE:, LANES:]),
-            jnp.where(even, top[:TILE], top[TILE:]),
-        )
-
-    @pl.loop(0, PAIRS)
+        parts = []
+        for head in (jnp.where(even, query, none), jnp.where(even, none, query)):
+            scores = lax.dot_general(
+                head, key_rows, (((1,), (1,)), ((), ())), preferred_element_type=F32
+            )
+            scores = scores + bias
+            highest = jnp.maximum(jnp.max(scores, axis=1, keepdims=True), FLOOR)
+            weights = jnp.exp(scores - highest).astype(BF16)
+            mixed = jnp.dot(weights, wide, preferred_element_type=F32)
+            parts.append(
+                (mixed[:, :LANES], mixed[:, LANES:], jnp.broadcast_to(highest, (TILE, LANES)))
+            )
+        return [jnp.where(even, first, second) for first, second in zip(*parts)]
+
+    @pl.loop(0, PAIRS, unroll=2)
     def _(pair):
         lanes = pl.ds(pl.multiple_of(pair * LANES, LANES), LANES)
-        near = pl.ds(2, 4)
+        near = pl.ds(0, NEAR_BLOCKS)
         key_rows = keys[near, :, lanes].reshape(ROWS, LANES)
         value_rows = values[near, :, lanes].reshape(ROWS, LANES)
         for tile in range(2):
             rows = pl.ds(tile * TILE, TILE)
-            mixed, total, top = attend(
-                tile, lanes, key_rows, value_rows, bias_near[rows, :]
-            )
+            mixed, total, top = attend(tile, lanes, key_rows, value_rows, bias_near[rows, :])
             acc_near[rows, lanes] = mixed
             sum_near[rows, lanes] = total
             max_near[rows, lanes] = top
-
-    for copy in own:
-        copy.wait_recv()
-
-    def project_slots(first, count):
-        project(arrived, first, count, wk, keys, NEAR_BLOCKS + first)
-        project(arrived, first, count, wv, values, NEAR_BLOCKS + first)
-
-    project_slots(1, 7)
 
     for copy in cross:
         copy.wait()
@@ -247,12 +237,12 @@
         far.append(copy)
     edges = [
         pltpu.make_async_remote_copy(
-            src_ref=normed.at[pl.ds(2, 2)], dst_ref=halo.at[pl.ds(0, 2)],
+            src_ref=normed.at[pl.ds(2, 2)], dst_ref=arrived.at[pl.ds(SLOTS, 2)],
             send_sem=send_halo.at[0], recv_sem=recv_halo.at[0],
             device_id=above, device_id_type=MESH,
         ),
         pltpu.make_async_remote_copy(
-            src_ref=normed.at[pl.ds(0, 2)], dst_ref=halo.at[pl.ds(2, 2)],
+            src_ref=normed.at[pl.ds(0, 2)], dst_ref=arrived.at[pl.ds(SLOTS + 2, 2)],
             send_sem=send_halo.at[1], recv_sem=recv_halo.at[1],
             device_id=below, device_id_type=MESH,
         ),
@@ -261,17 +251,18 @@
         copy.start()
     arrived[8] = far_rows(g)
 
+    def project_slots(first, count):
+        project(arrived, first, count, ((wk, keys), (wv, values)), NEAR_BLOCKS + first)
+
+    for copy in own:
+        copy.wait_recv()
+    project_slots(1, 7)
     for flow in (6, 0, 1, 2, 3):
         far[flow].wait_recv()
     project_slots(8, 6)
-    for copy in edges:
+    for copy in (far[4], far[5], *edges):
         copy.wait_recv()
-    for weight, dst in ((wk, keys), (wv, values)):
-        project(halo, 0, 2, weight, dst, 0)
-        project(halo, 2, 2, weight, dst, 6)
-    for flow in (4, 5):
-        far[flow].wait_recv()
-    project_slots(14, 2)
+    project_slots(14, 6)
 
     def slot_start(tile, entry):
         peer = peers_ref[tile, entry]
@@ -281,19 +272,19 @@
         turn = lax.rem(peer + core, 2)
         return NEAR_BLOCKS + 8 * other + 2 * place + turn
 
-    for tile in range(2):
-        rows = pl.ds(tile * TILE, TILE)
-        edge = pl.ds(6 * tile, 2)
-        starts = [slot_start(tile, entry) for entry in range(MAXLONG)]
-
-        @pl.loop(0, PAIRS)
-        def _(pair):
-            lanes = pl.ds(pl.multiple_of(pair * LANES, LANES), LANES)
+    starts = [[slot_start(tile, entry) for entry in range(MAXLONG)] for tile in range(2)]
+
+    @pl.loop(0, PAIRS, unroll=2)
+    def _(pair):
+        lanes = pl.ds(pl.multiple_of(pair * LANES, LANES), LANES)
+        for tile in range(2):
+            rows = pl.ds(tile * TILE, TILE)
+            edge = pl.ds(HALO + 2 * tile, 2)
 
             def gathered(ref):
                 return jnp.concatenate(
                     [ref[edge, :, lanes].reshape(TILE, LANES)]
-                    + [ref[start, :, lanes] for start in starts],
+                    + [ref[start, :, lanes] for start in starts[tile]],
                     axis=0,
                 )
 
@@ -310,9 +301,9 @@
 
     loads[4].wait()
 
-    @pl.loop(0, D // 256)
+    @pl.loop(0, 2, unroll=True)
     def _(step):
-        columns = pl.ds(pl.multiple_of(step * 256, 256), 256)
+        columns = pl.ds(pl.multiple_of(step * (D // 2), D // 2), D // 2)
         total = jnp.dot(attended[...], wo[:, columns], preferred_element_type=F32)
         out_ref[:, columns] = (feat[:, columns].astype(F32) + total).astype(BF16)
 
@@ -350,13 +341,12 @@
             pltpu.VMEM((4, PORTAL, D), BF16),
             pltpu.VMEM((4, PORTAL, D), BF16),
             pltpu.SMEM((1, 16), jnp.int32),
-            pltpu.VMEM((4, PORTAL, D), BF16),
-            pltpu.VMEM((16, PORTAL, D), BF16),
+            pltpu.VMEM((SLOTS + 4, PORTAL, D), BF16),
             pltpu.VMEM((flows, PORTAL, D), BF16),
             pltpu.VMEM((flows, PORTAL, D), BF16),
             pltpu.VMEM((4, PORTAL, D), BF16),
-            pltpu.VMEM((NEAR_BLOCKS + 16, PORTAL, D), BF16),
-            pltpu.VMEM((NEAR_BLOCKS + 16, PORTAL, D), BF16),
+            pltpu.VMEM((HALO + 4, PORTAL, D), BF16),
+            pltpu.VMEM((HALO + 4, PORTAL, D), BF16),
             pltpu.VMEM((ROWS, D), BF16),
             pltpu.VMEM((ROWS, ROWS), F32),
             pltpu.VMEM((2, TILE, TILE + MAXLONG * PORTAL), F32),

time: 62.4 us -> 53.9 us (0.86)
  the two profiles are of different devices: /device:TPU:17 before, /device:TPU:1 now
where the time goes in v1:
time: 53.9 us; the launch traced here: 53.7 us
  Pallas kernels  51.2 us (95%)
  local copies, waits for them, and re-layouts  1.87 us (3%)
  between operations  0.66 us (1%)
    pallas_call x1, Pallas kernels, local(): pl.pallas_call(kernel, name='layer', out_shape=jax.ShapeDtypeStruct((ROWS...  51.2 us
    unnamed x1, local copies, waits for them, and re-layouts  1.87 us

profile of v1, /device:TPU:1, one launch (start us, length us, event | category | flops | bytes accessed | tf_op | source)
XLA Modules:
  0.0 53.7 jit_solution(16606363325580695584)
XLA Ops:
  0.7 51.2 %layer.1 = bf16[256,1024]{1,0:T(8,128)(2,1)} custom-call(s32[1]{0:T(128)S(6)} %copy.11.reach_ref, s32[2,6]{1,0:T(2,128)} %peers_ref.1, s32[2]{0:T(128)} %count_ref.1, s32[1,16]{1,0:T(1,128)} %pick_ref.1, bf16[256,1024]{1,0:T(8,128)(2,1)} %feat_hbm.1, bf16[1024,1024]{1,0:T(8,128)(2,1)} %wq_hbm.1, bf16[1024,1024]{1,0:T(8,128)(2,1)} %wk_hbm.1, ...), custom_call_target="tpu_custom_call" | custom-call | tf_op jit(solution)/shard_map/layer/pallas_call | solution.py:329
  51.9 1.9 %copy.12 = bf16[256,1024]{1,0:T(8,128)(2,1)} copy(bf16[256,1024]{1,0:T(8,128)(2,1)} %layer.1) | data formatting | bytes 1048576

commit v2 on v1

--- a/solution.py
+++ b/solution.py
@@ -87,6 +87,7 @@
     recv_y,
     send_halo,
     recv_halo,
+    ready,
 ):
     g = lax.axis_index("grp")
     r = lax.axis_index("rng")
@@ -111,10 +112,16 @@
     for load in loads:
         load.start()
 
+    odd = lax.rem(r, 2)
     barrier = pltpu.get_barrier_semaphore()
-    friends = [device(dx, 0, dc) for dx, dc in row_flows] + [device(0, 1, 0), above, below]
+    friends = [device(dx, 0, dc) for dx, dc in row_flows] + [device(0, 1, 0)]
     for friend in friends:
         pl.semaphore_signal(barrier, inc=1, device_id=friend, device_id_type=MESH)
+
+    @pl.when(odd == 0)
+    def _():
+        for neighbour in (above, below):
+            pl.semaphore_signal(barrier, inc=1, device_id=neighbour, device_id_type=MESH)
 
     loads[0].wait()
 
@@ -136,7 +143,14 @@
     for flow in range(len(row_flows)):
         pick_own(flow)
 
-    pl.semaphore_wait(barrier, len(friends))
+    pl.semaphore_wait(barrier, len(friends) + 2 * odd)
+
+    @pl.when(odd == 1)
+    def _():
+        for side, neighbour in enumerate((above, below)):
+            pl.semaphore_signal(
+                ready.at[side], inc=1, device_id=neighbour, device_id_type=MESH
+            )
 
     cross = [
         pltpu.make_async_remote_copy(
@@ -247,8 +261,16 @@
             device_id=below, device_id_type=MESH,
         ),
     ]
-    for copy in edges:
-        copy.start()
+    @pl.when(odd == 0)
+    def _():
+        for side in range(2):
+            pl.semaphore_wait(ready.at[side], 1)
+
+    @pl.when(r != 0)
+    def _():
+        for copy in edges:
+            copy.start()
+
     arrived[8] = far_rows(g)
 
     def project_slots(first, count):
@@ -257,6 +279,11 @@
     for copy in own:
         copy.wait_recv()
     project_slots(1, 7)
+    @pl.when(r == 0)
+    def _():
+        for copy in edges:
+            copy.start()
+
     for flow in (6, 0, 1, 2, 3):
         far[flow].wait_recv()
     project_slots(8, 6)
@@ -362,6 +389,7 @@
             dma((2,)),
             dma((2,)),
             dma((2,)),
+            pltpu.SemaphoreType.REGULAR((2,)),
         ],
         compiler_params=pltpu.CompilerParams(
             collective_id=0, has_side_effects=True, vmem_limit_bytes=60 * 1024 * 1024

time: 53.9 us -> 45.7 us (0.85)
  Pallas kernels: 51.2 us -> 43 us
    pallas_call x1, Pallas kernels: 51.2 us -> 43 us  [local(): pl.pallas_call(kernel, name='layer', out_shape=jax.ShapeDtypeStruct((ROWS...]
where the time goes in v2:
time: 45.7 us; the launch traced here: 45.5 us
  Pallas kernels  43 us (94%)
  local copies, waits for them, and re-layouts  1.87 us (4%)
  between operations  0.66 us (1%)
    pallas_call x1, Pallas kernels, local(): pl.pallas_call(kernel, name='layer', out_shape=jax.ShapeDtypeStruct((ROWS...  43 us
    unnamed x1, local copies, waits for them, and re-layouts  1.87 us

profile of v2, /device:TPU:1, one launch (start us, length us, event | category | flops | bytes accessed | tf_op | source)
XLA Modules:
  0.0 45.5 jit_solution(13147590778983432575)
XLA Ops:
  0.7 43.0 %layer.1 = bf16[256,1024]{1,0:T(8,128)(2,1)} custom-call(s32[1]{0:T(128)S(6)} %copy.11.reach_ref, s32[2,6]{1,0:T(2,128)} %peers_ref.1, s32[2]{0:T(128)} %count_ref.1, s32[1,16]{1,0:T(1,128)} %pick_ref.1, bf16[256,1024]{1,0:T(8,128)(2,1)} %feat_hbm.1, bf16[1024,1024]{1,0:T(8,128)(2,1)} %wq_hbm.1, bf16[1024,1024]{1,0:T(8,128)(2,1)} %wk_hbm.1, ...), custom_call_target="tpu_custom_call" | custom-call | tf_op jit(solution)/shard_map/layer/pallas_call | solution.py:356
  43.6 1.9 %copy.12 = bf16[256,1024]{1,0:T(8,128)(2,1)} copy(bf16[256,1024]{1,0:T(8,128)(2,1)} %layer.1) | data formatting | bytes 1048576

commit v3 on v2

--- a/solution.py
+++ b/solution.py
@@ -48,21 +48,23 @@
 
 
 def kernel(
+    reach_hbm,
+    peers_hbm,
+    count_hbm,
+    pick_hbm,
+    feat_hbm,
+    wq_hbm,
+    wk_hbm,
+    wv_hbm,
+    out_ref,
     reach_ref,
     peers_ref,
     count_ref,
     pick_ref,
-    feat_hbm,
-    wq_hbm,
-    wk_hbm,
-    wv_hbm,
-    wo_hbm,
-    out_ref,
     feat,
     wq,
     wk,
     wv,
-    wo,
     normed,
     partner,
     partner_pick,
@@ -72,7 +74,6 @@
     queries,
     keys,
     values,
-    attended,
     bias_near,
     bias_far,
     acc_near,
@@ -103,13 +104,22 @@
     below = (g, lax.rem(r + 15, 16))
     row_flows = X_ORDER + ((0, 1),)
 
-    loads = [
-        pltpu.make_async_copy(src, dst, in_sem.at[i])
-        for i, (src, dst) in enumerate(
-            ((feat_hbm, feat), (wq_hbm, wq), (wk_hbm, wk), (wv_hbm, wv), (wo_hbm, wo))
-        )
-    ]
-    for load in loads:
+    def loads_of(first, *pairs):
+        return [
+            pltpu.make_async_copy(src, dst, in_sem.at[first + i])
+            for i, (src, dst) in enumerate(pairs)
+        ]
+
+    feat_load, pick_load, *small_loads = loads_of(
+        0,
+        (feat_hbm, feat),
+        (pick_hbm, pick_ref),
+        (reach_hbm, reach_ref),
+        (peers_hbm, peers_ref),
+        (count_hbm, count_ref),
+    )
+    loads = loads_of(5, (wq_hbm, wq), (wk_hbm, wk), (wv_hbm, wv))
+    for load in (feat_load, pick_load, *small_loads):
         load.start()
 
     odd = lax.rem(r, 2)
@@ -123,7 +133,9 @@
         for neighbour in (above, below):
             pl.semaphore_signal(barrier, inc=1, device_id=neighbour, device_id_type=MESH)
 
-    loads[0].wait()
+    feat_load.wait()
+    for load in loads:
+        load.start()
 
     @pl.loop(0, ROWS // PORTAL)
     def _(block):
@@ -132,17 +144,10 @@
         factor = lax.rsqrt(jnp.mean(widened * widened, axis=1, keepdims=True) + EPSILON)
         normed[block] = (widened * factor).astype(BF16)
 
-    def pick_own(flow):
-        dx, dc = row_flows[flow]
-        target, _ = device(dx, 0, dc)
-        stage_own[flow] = normed[pick_ref[0, target]]
-
     def slot_of_flow(dx, dc, far):
         return 8 * far + 2 * GRAY[dx] + dc
 
-    for flow in range(len(row_flows)):
-        pick_own(flow)
-
+    pick_load.wait()
     pl.semaphore_wait(barrier, len(friends) + 2 * odd)
 
     @pl.when(odd == 1)
@@ -166,6 +171,8 @@
         copy.start()
     own = []
     for flow, (dx, dc) in enumerate(row_flows):
+        target, _ = device(dx, 0, dc)
+        stage_own[flow] = normed[pick_ref[0, target]]
         copy = pltpu.make_async_remote_copy(
             src_ref=stage_own.at[flow],
             dst_ref=arrived.at[slot_of_flow(dx, dc, 0)],
@@ -177,6 +184,8 @@
         copy.start()
         own.append(copy)
 
+    for load in small_loads:
+        load.wait()
     reach = reach_ref[0]
     place_q = lax.broadcasted_iota(jnp.int32, (ROWS, ROWS), 0)
     place_k = lax.broadcasted_iota(jnp.int32, (ROWS, ROWS), 1)
@@ -189,10 +198,10 @@
         bias_far[tile, :, :TILE] = jnp.where(gap <= reach, 0.0, -jnp.inf)
         bias_far[tile, :, TILE:] = jnp.where(slot_of < count_ref[tile], 0.0, -jnp.inf)
 
+    loads[0].wait()
+    project(normed, 0, 4, ((wq, queries),), 0, SCALE)
     loads[1].wait()
-    project(normed, 0, 4, ((wq, queries),), 0, SCALE)
     loads[2].wait()
-    loads[3].wait()
     project(normed, 0, 4, ((wk, keys), (wv, values)), 0)
 
     even = lax.broadcasted_iota(jnp.int32, (TILE, LANES), 1) < LANES // 2
@@ -238,7 +247,6 @@
     for flow, (dx, dc) in enumerate(row_flows):
         target, _ = device(dx, 0, dc)
         stage_far[flow] = far_rows(target)
-    for flow, (dx, dc) in enumerate(row_flows):
         copy = pltpu.make_async_remote_copy(
             src_ref=stage_far.at[flow],
             dst_ref=arrived.at[slot_of_flow(dx, dc, 1)],
@@ -301,7 +309,7 @@
 
     starts = [[slot_start(tile, entry) for entry in range(MAXLONG)] for tile in range(2)]
 
-    @pl.loop(0, PAIRS, unroll=2)
+    @pl.loop(0, PAIRS, unroll=4)
     def _(pair):
         lanes = pl.ds(pl.multiple_of(pair * LANES, LANES), LANES)
         for tile in range(2):
@@ -324,15 +332,7 @@
             far_part = jnp.exp(top - highest)
             mixed = acc_near[rows, lanes] * near_part + mixed * far_part
             total = sum_near[rows, lanes] * near_part + total * far_part
-            attended[rows, lanes] = (mixed / total).astype(BF16)
-
-    loads[4].wait()
-
-    @pl.loop(0, 2, unroll=True)
-    def _(step):
-        columns = pl.ds(pl.multiple_of(step * (D // 2), D // 2), D // 2)
-        total = jnp.dot(attended[...], wo[:, columns], preferred_element_type=F32)
-        out_ref[:, columns] = (feat[:, columns].astype(F32) + total).astype(BF16)
+            out_ref[rows, lanes] = (mixed / total).astype(BF16)
 
     for copy in own + far + edges:
         copy.wait_send()
@@ -349,19 +349,21 @@
     long_count,
     send_tile,
 ):
-    smem = pl.BlockSpec(memory_space=pltpu.SMEM)
-    hbm = pl.BlockSpec(memory_space=pl.ANY)
+    hbm = pl.BlockSpec(memory_space=pltpu.HBM)
     flows = len(X_ORDER) + 1
     dma = pltpu.SemaphoreType.DMA
-    return pl.pallas_call(
+    attended = pl.pallas_call(
         kernel,
         name="layer",
         out_shape=jax.ShapeDtypeStruct((ROWS, D), BF16),
-        in_specs=[smem] * 4 + [hbm] * 5,
+        in_specs=[hbm] * 8,
         out_specs=pl.BlockSpec(memory_space=pltpu.VMEM),
         scratch_shapes=[
+            pltpu.SMEM((1,), jnp.int32),
+            pltpu.SMEM((2, MAXLONG), jnp.int32),
+            pltpu.SMEM((2,), jnp.int32),
+            pltpu.SMEM((1, 16), jnp.int32),
             pltpu.VMEM((ROWS, D), BF16),
-            pltpu.VMEM((D, D), BF16),
             pltpu.VMEM((D, D), BF16),
             pltpu.VMEM((D, D), BF16),
             pltpu.VMEM((D, D), BF16),
@@ -374,13 +376,12 @@
             pltpu.VMEM((4, PORTAL, D), BF16),
             pltpu.VMEM((HALO + 4, PORTAL, D), BF16),
             pltpu.VMEM((HALO + 4, PORTAL, D), BF16),
-            pltpu.VMEM((ROWS, D), BF16),
             pltpu.VMEM((ROWS, ROWS), F32),
             pltpu.VMEM((2, TILE, TILE + MAXLONG * PORTAL), F32),
             pltpu.VMEM((ROWS, D), F32),
             pltpu.VMEM((ROWS, D), F32),
             pltpu.VMEM((ROWS, D), F32),
-            dma((5,)),
+            dma((8,)),
             dma((flows,)),
             dma((flows,)),
             dma((flows,)),
@@ -392,7 +393,7 @@
             pltpu.SemaphoreType.REGULAR((2,)),
         ],
         compiler_params=pltpu.CompilerParams(
-            collective_id=0, has_side_effects=True, vmem_limit_bytes=60 * 1024 * 1024
+            collective_id=0, has_side_effects=True, vmem_limit_bytes=56 * 1024 * 1024
         ),
     )(
         band_reach,
@@ -403,8 +404,9 @@
         query_weight,
         key_weight,
         value_weight,
-        out_weight,
     )
+    projected = jnp.dot(attended, out_weight, preferred_element_type=F32)
+    return (features.astype(F32) + projected).astype(BF16)
 
 
 def solution(mesh):

time: 45.7 us -> 44.7 us (0.978)
  matrix products: 0 us -> 2.55 us
  local copies, waits for them, and re-layouts: 1.87 us -> 0.01 us
  Pallas kernels: 43 us -> 41.2 us
    dot_general x0 -> x1, matrix products: none -> 2.55 us  [local(): projected = jnp.dot(attended, out_weight, preferred_element_type=F32)]
    unnamed x1 -> x4, local copies, waits for them, and re-layouts: 1.87 us -> 0.01 us
    pallas_call x1, Pallas kernels: 43 us -> 41.2 us  [local(): pl.pallas_call(kernel, name='layer', out_shape=jax.ShapeDtypeStruct((ROWS...]
where the time goes in v3:
time: 44.7 us; the launch traced here: 44.5 us
  Pallas kernels  41.2 us (92%)
  matrix products  2.55 us (6%)
  between operations  0.83 us (2%)
    pallas_call x1, Pallas kernels, local(): pl.pallas_call(kernel, name='layer', out_shape=jax.ShapeDtypeStruct((ROWS...  41.2 us
    dot_general x1, matrix products, local(): projected = jnp.dot(attended, out_weight, preferred_element_type=F32)  2.55 us

profile of v3, /device:TPU:1, one launch (start us, length us, event | category | flops | bytes accessed | tf_op | source)
XLA Modules:
  0.0 44.5 jit_solution(11720045298432496017)
XLA Ops:
  0.0 0.0 copy-start
  0.8 0.0 copy-start.1
  0.8 41.2 %layer.1 = bf16[256,1024]{1,0:T(8,128)(2,1)} custom-call(s32[1]{0:T(128)S(6)} %copy.10.reach_hbm, s32[2,6]{1,0:T(2,128)} %peers_hbm.1, s32[2]{0:T(128)} %count_hbm.1, s32[1,16]{1,0:T(1,128)} %pick_hbm.1, bf16[256,1024]{1,0:T(8,128)(2,1)} %feat_hbm.1, bf16[1024,1024]{1,0:T(8,128)(2,1)} %wq_hbm.1, bf16[1024,1024]{1,0:T(8,128)(2,1)} %wk_hbm.1, ...), custom_call_target="tpu_custom_call" | custom-call | tf_op jit(solution)/shard_map/layer/pallas_call | solution.py:355
  42.0 0.0 copy-done
  42.0 0.0 copy-done.1
  42.0 2.5 %fusion = bf16[256,1024]{1,0:T(8,128)(2,1)} fusion(bf16[256,1024]{1,0:T(8,128)(2,1)} %layer.1, bf16[1024,1024]{1,0:T(8,128)(2,1)S(1)} %copy-done, bf16[256,1024]{1,0:T(8,128)(2,1)S(1)} %copy-done.1), kind=kOutput, calls=%fused_computation.1 | convolution fusion | flops 537657344 | bytes 3670016 | tf_op jit(solution)/shard_map/dot_general | solution.py:408
Async XLA Ops:
  0.0 42.0 %copy-start = (bf16[1024,1024]{1,0:T(8,128)(2,1)S(1)}, bf16[1024,1024]{1,0:T(8,128)(2,1)}, u32[]{:S(2)}) copy-start(bf16[1024,1024]{1,0:T(8,128)(2,1)} %param.13) | copy-start | bytes 6291460
  0.8 41.2 %copy-start.1 = (bf16[256,1024]{1,0:T(8,128)(2,1)S(1)}, bf16[256,1024]{1,0:T(8,128)(2,1)}, u32[]{:S(2)}) copy-start(bf16[256,1024]{1,0:T(8,128)(2,1)} %feat_hbm.1) | copy-start | bytes 1572868

commit v4 on v3

--- a/solution.py
+++ b/solution.py
@@ -48,7 +48,7 @@
 
 
 def kernel(
-    reach_hbm,
+    reach_ref,
     peers_hbm,
     count_hbm,
     pick_hbm,
@@ -57,7 +57,6 @@
     wk_hbm,
     wv_hbm,
     out_ref,
-    reach_ref,
     peers_ref,
     count_ref,
     pick_ref,
@@ -114,11 +113,10 @@
         0,
         (feat_hbm, feat),
         (pick_hbm, pick_ref),
-        (reach_hbm, reach_ref),
         (peers_hbm, peers_ref),
         (count_hbm, count_ref),
     )
-    loads = loads_of(5, (wq_hbm, wq), (wk_hbm, wk), (wv_hbm, wv))
+    loads = loads_of(4, (wq_hbm, wq), (wk_hbm, wk), (wv_hbm, wv))
     for load in (feat_load, pick_load, *small_loads):
         load.start()
 
@@ -355,11 +353,10 @@
     attended = pl.pallas_call(
         kernel,
         name="layer",
-        out_shape=jax.ShapeDtypeStruct((ROWS, D), BF16),
-        in_specs=[hbm] * 8,
+        out_shape=pltpu.VMEM((ROWS, D), BF16),
+        in_specs=[pl.BlockSpec(memory_space=pltpu.SMEM)] + [hbm] * 7,
         out_specs=pl.BlockSpec(memory_space=pltpu.VMEM),
         scratch_shapes=[
-            pltpu.SMEM((1,), jnp.int32),
             pltpu.SMEM((2, MAXLONG), jnp.int32),
             pltpu.SMEM((2,), jnp.int32),
             pltpu.SMEM((1, 16), jnp.int32),
@@ -381,7 +378,7 @@
             pltpu.VMEM((ROWS, D), F32),
             pltpu.VMEM((ROWS, D), F32),
             pltpu.VMEM((ROWS, D), F32),
-            dma((8,)),
+            dma((7,)),
             dma((flows,)),
             dma((flows,)),
             dma((flows,)),
@@ -393,17 +390,22 @@
             pltpu.SemaphoreType.REGULAR((2,)),
         ],
         compiler_params=pltpu.CompilerParams(
-            collective_id=0, has_side_effects=True, vmem_limit_bytes=56 * 1024 * 1024
+            collective_id=0, has_side_effects=True, vmem_limit_bytes=50 * 1024 * 1024
         ),
     )(
         band_reach,
-        long_peers,
-        long_count,
-        send_tile,
-        features,
-        query_weight,
-        key_weight,
-        value_weight,
+        *(
+            pltpu.with_memory_space_constraint(operand, pltpu.HBM)
+            for operand in (
+                long_peers,
+                long_count,
+                send_tile,
+                features,
+                query_weight,
+                key_weight,
+                value_weight,
+            )
+        )
     )
     projected = jnp.dot(attended, out_weight, preferred_element_type=F32)
     return (features.astype(F32) + projected).astype(BF16)

time: 44.7 us -> 42.7 us (0.955)
  matrix products: 2.55 us -> 1.51 us
  Pallas kernels: 41.2 us -> 40.3 us
    dot_general x1, matrix products: 2.55 us -> 1.51 us  [local(): projected = jnp.dot(attended, out_weight, preferred_element_type=F32)]
    pallas_call x1, Pallas kernels: 41.2 us -> 40.3 us  [local(): pl.pallas_call(kernel, name='layer', out_shape=pltpu.VMEM((ROWS, D), BF16...]
where the time goes in v4:
time: 42.7 us; the launch traced here: 42.6 us
  Pallas kernels  40.3 us (94%)
  matrix products  1.51 us (4%)
  between operations  0.83 us (2%)
    pallas_call x1, Pallas kernels, local(): pl.pallas_call(kernel, name='layer', out_shape=pltpu.VMEM((ROWS, D), BF16...  40.3 us
    dot_general x1, matrix products, local(): projected = jnp.dot(attended, out_weight, preferred_element_type=F32)  1.51 us

profile of v4, /device:TPU:1, one launch (start us, length us, event | category | flops | bytes accessed | tf_op | source)
XLA Modules:
  0.0 42.6 jit_solution(8265696605024323800)
XLA Ops:
  0.0 0.0 copy-start
  0.8 0.0 copy-start.1
  0.8 40.3 %layer.1 = bf16[256,1024]{1,0:T(8,128)(2,1)S(1)} custom-call(s32[1]{0:T(128)S(6)} %copy.10.reach_ref, s32[2,6]{1,0:T(2,128)} %peers_hbm.1, s32[2]{0:T(128)} %count_hbm.1, s32[1,16]{1,0:T(1,128)} %pick_hbm.1, bf16[256,1024]{1,0:T(8,128)(2,1)} %feat_hbm.1, bf16[1024,1024]{1,0:T(8,128)(2,1)} %wq_hbm.1, bf16[1024,1024]{1,0:T(8,128)(2,1)} %wk_hbm.1, ...), custom_call_target="tpu_custom_call" | custom-call | tf_op jit(solution)/shard_map/layer/pallas_call | solution.py:353
  41.1 0.0 copy-done
  41.1 0.0 copy-done.1
  41.1 1.5 %fusion = bf16[256,1024]{1,0:T(8,128)(2,1)} fusion(bf16[256,1024]{1,0:T(8,128)(2,1)S(1)} %layer.1, bf16[1024,1024]{1,0:T(8,128)(2,1)S(1)} %copy-done, bf16[256,1024]{1,0:T(8,128)(2,1)S(1)} %copy-done.1), kind=kOutput, calls=%fused_computation.1 | convolution fusion | flops 537657344 | bytes 3670016 | tf_op jit(solution)/shard_map/dot_general | solution.py:410
Async XLA Ops:
  0.0 41.1 %copy-start = (bf16[1024,1024]{1,0:T(8,128)(2,1)S(1)}, bf16[1024,1024]{1,0:T(8,128)(2,1)}, u32[]{:S(2)}) copy-start(bf16[1024,1024]{1,0:T(8,128)(2,1)} %param.13) | copy-start | bytes 6291460
  0.8 40.3 %copy-start.1 = (bf16[256,1024]{1,0:T(8,128)(2,1)S(1)}, bf16[256,1024]{1,0:T(8,128)(2,1)}, u32[]{:S(2)}) copy-start(bf16[256,1024]{1,0:T(8,128)(2,1)} %feat_hbm.1) | copy-start | bytes 1572868

commit v5 on v4

--- a/solution.py
+++ b/solution.py
@@ -307,7 +307,7 @@
 
     starts = [[slot_start(tile, entry) for entry in range(MAXLONG)] for tile in range(2)]
 
-    @pl.loop(0, PAIRS, unroll=4)
+    @pl.loop(0, PAIRS, unroll=True)
     def _(pair):
         lanes = pl.ds(pl.multiple_of(pair * LANES, LANES), LANES)
         for tile in range(2):

time: 42.7 us -> 41.9 us (0.981)
  Pallas kernels: 40.3 us -> 39.5 us
    pallas_call x1, Pallas kernels: 40.3 us -> 39.5 us  [local(): pl.pallas_call(kernel, name='layer', out_shape=pltpu.VMEM((ROWS, D), BF16...]
where the time goes in v5:
time: 41.9 us; the launch traced here: 41.8 us
  Pallas kernels  39.5 us (94%)
  matrix products  1.51 us (4%)
  between operations  0.83 us (2%)
    pallas_call x1, Pallas kernels, local(): pl.pallas_call(kernel, name='layer', out_shape=pltpu.VMEM((ROWS, D), BF16...  39.5 us
    dot_general x1, matrix products, local(): projected = jnp.dot(attended, out_weight, preferred_element_type=F32)  1.51 us

profile of v5, /device:TPU:1, one launch (start us, length us, event | category | flops | bytes accessed | tf_op | source)
XLA Modules:
  0.0 41.8 jit_solution(364226639434758517)
XLA Ops:
  0.0 0.0 copy-start
  0.8 0.0 copy-start.1
  0.8 39.5 %layer.1 = bf16[256,1024]{1,0:T(8,128)(2,1)S(1)} custom-call(s32[1]{0:T(128)S(6)} %copy.10.reach_ref, s32[2,6]{1,0:T(2,128)} %peers_hbm.1, s32[2]{0:T(128)} %count_hbm.1, s32[1,16]{1,0:T(1,128)} %pick_hbm.1, bf16[256,1024]{1,0:T(8,128)(2,1)} %feat_hbm.1, bf16[1024,1024]{1,0:T(8,128)(2,1)} %wq_hbm.1, bf16[1024,1024]{1,0:T(8,128)(2,1)} %wk_hbm.1, ...), custom_call_target="tpu_custom_call" | custom-call | tf_op jit(solution)/shard_map/layer/pallas_call | solution.py:353
  40.3 0.0 copy-done
  40.3 0.0 copy-done.1
  40.3 1.5 %fusion = bf16[256,1024]{1,0:T(8,128)(2,1)} fusion(bf16[256,1024]{1,0:T(8,128)(2,1)S(1)} %layer.1, bf16[1024,1024]{1,0:T(8,128)(2,1)S(1)} %copy-done, bf16[256,1024]{1,0:T(8,128)(2,1)S(1)} %copy-done.1), kind=kOutput, calls=%fused_computation.1 | convolution fusion | flops 537657344 | bytes 3670016 | tf_op jit(solution)/shard_map/dot_general | solution.py:410
Async XLA Ops:
  0.0 40.3 %copy-start = (bf16[1024,1024]{1,0:T(8,128)(2,1)S(1)}, bf16[1024,1024]{1,0:T(8,128)(2,1)}, u32[]{:S(2)}) copy-start(bf16[1024,1024]{1,0:T(8,128)(2,1)} %param.13) | copy-start | bytes 6291460
  0.8 39.5 %copy-start.1 = (bf16[256,1024]{1,0:T(8,128)(2,1)S(1)}, bf16[256,1024]{1,0:T(8,128)(2,1)}, u32[]{:S(2)}) copy-start(bf16[256,1024]{1,0:T(8,128)(2,1)} %feat_hbm.1) | copy-start | bytes 1572868
